TPU v7x, 32 devices: a whole 2x2x4 slice. The times are simulated.
32 devices in a mesh: row: 4 (over x, core), col: 8 (over z, y).
Axes of the slice: x: 2, y: 2, z: 4, core: 2. Of those that a mesh axis runs over, the one named last changes fastest.
Arguments:
- pooled: bfloat16 [2048, 1152], P(('row', 'col')), may hold values from -32 to 32
- hidden: bfloat16 [2048, 4304], P(('row', 'col')), may hold values from -6 to 6
- text: bfloat16 [2048, 1152], P(('row', 'col')), may hold values from -12 to 12
- weight: float32 [1152, 4304], P('col', 'row'), may hold values from -0.09375 to 0.09375
- row_moment: float32 [1152], P('col'), may hold values from 1e-07 to 1e-05
- col_moment: float32 [4304], P('row'), may hold values from 1e-07 to 1e-05
- log_scale: float32 [], replicated, may hold values from 4.2 to 4.8
- bias: float32 [], replicated, may hold values from -16 to -12
Outputs:
- update: float32 [1152, 4304], P('col', 'row')
- new_row: float32 [1152], P('col')
- new_col: float32 [4304], P('row')
- loss: float32 [], replicated
All inputs are finite; a program needn't handle non-finite values.
Results may differ from a plain program's by a relative error of at most 0.004.
Values may be sent and summed in bfloat16 or wider, within the bound.
A program may use at most 128 MiB of HBM per device.

v0:
```python
import jax
import jax.numpy as jnp
from jax import lax
from jax.sharding import PartitionSpec as P

D = 1152
FF = 4304
EPSILON = 1e-06
DECAY_RATE = 0.8
CLIP_LEVEL = 1.0
FLOOR_VALUE = 1e-30


def over_row_index(positions, column, tokens, columns):
    return (positions // tokens * columns + column) * tokens + positions % tokens


def over_col_index(positions, row_place, tokens, columns):
    return row_place * columns * tokens + positions


def pair_tile(images, image_ids, texts, text_ids, logit_scale, bias, batch_total):
    logits = logit_scale * jnp.dot(images, texts.T, preferred_element_type=jnp.float32) + bias
    label_sign = jnp.where(
        image_ids[:, None] == text_ids[None, :], jnp.float32(1.0), jnp.float32(-1.0)
    )
    loss_sum = jnp.sum(jax.nn.softplus(-label_sign * logits))
    grad_logits = (-label_sign * jax.nn.sigmoid(-label_sign * logits) / batch_total).astype(
        jnp.bfloat16
    )
    return (loss_sum, logit_scale * jnp.dot(grad_logits, texts, preferred_element_type=jnp.float32))


def per_device(pooled, hidden, text, weight, row_moment, col_moment, log_scale, bias):
    rows_count = lax.axis_size("row")
    cols_count = lax.axis_size("col")
    row_place = lax.axis_index("row")
    col_place = lax.axis_index("col")
    tokens = pooled.shape[0]
    batch_total = tokens * rows_count * cols_count
    split_hidden = lax.all_to_all(hidden, "row", split_axis=1, concat_axis=0, tiled=True)
    hidden_cols = split_hidden.shape[1]
    weight_half = weight.astype(jnp.bfloat16)
    grouped = split_hidden.reshape(rows_count, tokens, hidden_cols)
    hidden_all = lax.all_gather(grouped, "col", axis=1, tiled=True).reshape(
        batch_total, hidden_cols
    )
    partial_proj = lax.dot_general(
        weight_half, hidden_all, (((1,), (1,)), ((), ())), preferred_element_type=jnp.float32
    )
    summed = lax.psum_scatter(partial_proj, "row", scatter_dimension=1, tiled=True)
    projected = lax.all_to_all(summed, "col", split_axis=1, concat_axis=0, tiled=True).T
    mixed_rows = pooled.astype(jnp.float32) + projected
    length = jnp.sqrt(jnp.sum(mixed_rows * mixed_rows, axis=1, keepdims=True) + EPSILON)
    image_unit = mixed_rows / length
    images = image_unit.astype(jnp.bfloat16)
    text_float = text.astype(jnp.float32)
    text_units = (
        text_float / jnp.sqrt(jnp.sum(text_float * text_float, axis=1, keepdims=True) + EPSILON)
    ).astype(jnp.bfloat16)
    logit_scale = jnp.exp(log_scale)
    image_rows = lax.all_gather(images, "row", axis=0, tiled=True)
    image_ids = over_row_index(
        jnp.arange(image_rows.shape[0], dtype=jnp.int32), col_place, tokens, cols_count
    )
    piece = lax.all_gather(text_units, "col", axis=0, tiled=True)
    text_ids = over_col_index(
        jnp.arange(piece.shape[0], dtype=jnp.int32), row_place, tokens, cols_count
    )
    loss_local, unit_part = pair_tile(
        image_rows, image_ids, piece, text_ids, logit_scale, bias, batch_total
    )
    unit_grad = lax.psum_scatter(unit_part, "row", scatter_dimension=0, tiled=True)
    mixed_grad = (
        (unit_grad - image_unit * jnp.sum(image_unit * unit_grad, axis=1, keepdims=True)) / length
    ).astype(jnp.bfloat16)
    grad_cols = lax.all_to_all(mixed_grad.T, "col", split_axis=0, concat_axis=1, tiled=True)
    gradient = jnp.dot(
        lax.all_gather(grad_cols, "row", axis=1, tiled=True),
        hidden_all,
        preferred_element_type=jnp.float32,
    )
    squared = gradient * gradient + FLOOR_VALUE
    row_sum = lax.psum(jnp.sum(squared, axis=1), "row")
    col_sum = lax.psum(jnp.sum(squared, axis=0), "col")
    new_row = DECAY_RATE * row_moment + (1.0 - DECAY_RATE) * row_sum / FF
    new_col = DECAY_RATE * col_moment + (1.0 - DECAY_RATE) * col_sum / D
    second = new_row[:, None] * new_col[None, :]
    raw_update = gradient / jnp.sqrt(second)
    loss_total = lax.psum(loss_local, ("row", "col"))
    update_total = lax.psum(jnp.sum(raw_update * raw_update), ("row", "col"))
    update_rms = jnp.sqrt(update_total / (D * FF))
    update = raw_update / jnp.maximum(1.0, update_rms / CLIP_LEVEL)
    loss = loss_total / batch_total
    return (update, new_row, new_col, loss)


def solution(mesh):
    return jax.shard_map(
        per_device,
        mesh=mesh,
        in_specs=(
            P(("row", "col"), None),
            P(("row", "col"), None),
            P(("row", "col"), None),
            P("col", "row"),
            P("col"),
            P("row"),
            P(),
            P(),
        ),
        out_specs=(P("col", "row"), P("col"), P("row"), P()),
        check_vma=False,
    )
```

profile of v0, /device:TPU:12, one launch (start us, length us, event | category | flops | bytes accessed | tf_op | source)
XLA Modules:
  0.0 324.7 jit_solution(10579943734243616240)
XLA Ops:
  7.2 0.0 all-gather.3.cloned.1.call-start
  7.2 1.5 all_to_all.40
  8.7 0.1 copy.22
  8.8 12.1 %all_to_all.54 = bf16[64,4,1076]{2,0,1:T(8,128)(2,1)S(1)} all-to-all(bf16[64,4,1076]{2,0,1:T(8,128)(2,1)S(1)} %copy.22), channel_id=1, replica_groups=mesh['row'=4,'col'=8] {'row'}, dimensions={1} | all-to-all | bytes 1101824 | tf_op jit(solution)/shard_map/all_to_all | solution.py:41
  20.9 1.3 copy.23
  22.1 0.0 all-gather.3.cloned.1.call-update
  22.2 0.0 reduce-scatter.3.cloned.1.call-start
  22.2 78.1 %all-gather.3.cloned.1.call-done = bf16[4,512,1076]{2,0,1:T(4,128)(2,1)} async-done(((bf16[4,64,1076]{2,0,1:T(4,128)(2,1)}), bf16[4,512,1076]{2,0,1:T(4,128)(2,1)}) %all-gather.3.cloned.1.call-update) | async-done | bytes 4407312 | tf_op jit(solution)/shard_map/all_gather | solution.py:45
  100.3 10.4 %copy.24 = bf16[4,512,1076]{1,0,2:T(4,128)(2,1)} copy(bf16[4,512,1076]{2,0,1:T(4,128)(2,1)} %all-gather.3.cloned.1.call-done) | data formatting | bytes 8814592 | tf_op jit(solution)/shard_map/all_gather | solution.py:45
  110.7 3.9 %pad = bf16[1080,4,512]{2,1,0:T(4,128)(2,1)S(1)} pad(bf16[1076,4,512]{2,1,0:T(4,128)(2,1)} %bitcast.38, bf16[]{:T(256)} %constant.79), padding=0_4x0_0x0_0 | pad | bytes 8830978
  114.6 0.0 copy-start.2
  114.6 1.9 copy.31
  116.5 0.0 copy-start
  116.5 2.0 copy-done
  118.5 0.0 copy-done.2
  118.5 2.2 fusion.6
  120.8 0.0 copy-start.3
  120.8 0.0 reduce-scatter.3.cloned.1.call-update
  120.8 0.0 all-gather.5.cloned.1.call-start
  120.9 0.8 copy-done.3
  121.7 0.1 fusion.8
  121.8 0.8 fusion.9
  122.6 0.0 all-gather.5.cloned.1.call-update
  122.6 23.8 %reduce-scatter.3.cloned.1.call-done = f32[144,512]{1,0:T(8,128)} async-done(((f32[144,2048]{1,0:T(8,128)}), f32[144,512]{1,0:T(8,128)}) %reduce-scatter.3.cloned.1.call-update) | async-done | bytes 294928 | tf_op jit(solution)/shard_map/reduce_scatter | solution.py:51
  146.4 2.0 copy.29
  148.3 6.1 %all-to-all-start.1 = ((f32[144,8,64]{0,2,1:T(8,128)}), f32[144,8,64]{0,2,1:T(8,128)S(1)}, u32[]{:S(2)}, u32[]{:S(2)}) async-start(f32[144,8,64]{0,2,1:T(8,128)} %bitcast.1), calls=%async_computation.2 | async-start | bytes 1048576 | tf_op jit(solution)/shard_map/all_to_all | solution.py:52
  154.4 0.0 copy-start.1
  154.4 0.0 reduce-scatter.5.cloned.1.call-start
  155.8 14.4 %all-to-all-done.1 = f32[144,8,64]{0,2,1:T(8,128)S(1)} async-done(((f32[144,8,64]{0,2,1:T(8,128)}), f32[144,8,64]{0,2,1:T(8,128)S(1)}, u32[]{:S(2)}, u32[]{:S(2)}) %all-to-all-start.1) | async-done | bytes 294944 | tf_op jit(solution)/shard_map/all_to_all | solution.py:52
  170.2 0.3 copy.26
  170.5 0.2 all_to_all.46
  170.7 0.0 copy-done.1
  170.7 0.1 multiply_reduce_fusion.2
  170.9 0.1 fusion.26
  171.0 7.1 %all_gather.13 = bf16[256,1152]{1,0:T(8,128)(2,1)S(1)} all-gather(bf16[64,1152]{1,0:T(8,128)(2,1)S(1)} %fusion.26), channel_id=1, replica_groups=mesh['row'=4,'col'=8] {'row'}, dimensions={0}, use_global_device_ids=true | all-gather | bytes 737280 | tf_op jit(solution)/shard_map/all_gather | solution.py:62
  178.1 12.6 %all-gather.5.cloned.1.call-done = bf16[512,1152]{1,0:T(8,128)(2,1)} async-done(((bf16[64,1152]{1,0:T(8,128)(2,1)}), bf16[512,1152]{1,0:T(8,128)(2,1)}) %all-gather.5.cloned.1.call-update) | async-done | bytes 1179664 | tf_op jit(solution)/shard_map/all_gather | solution.py:66
  190.6 0.0 copy-start.8
  190.6 2.9 fusion.5
  193.5 0.0 copy-done.8
  193.5 1.6 convolution_multiply_fusion
  195.1 0.0 reduce-scatter.5.cloned.1.call-update
  195.1 26.1 %reduce-scatter.5.cloned.1.call-done = f32[64,1152]{1,0:T(8,128)} async-done(((f32[256,1152]{1,0:T(8,128)}), f32[64,1152]{1,0:T(8,128)}) %reduce-scatter.5.cloned.1.call-update) | async-done | bytes 294928 | tf_op jit(solution)/shard_map/reduce_scatter | solution.py:73
  221.2 1.2 multiply_reduce_fusion.1
  222.4 1.1 fusion.16
  223.5 0.4 all_to_all.47
  223.9 12.6 %all_to_all.55 = bf16[8,144,64]{1,2,0:T(8,128)(2,1)S(1)} all-to-all(bf16[8,144,64]{1,2,0:T(8,128)(2,1)S(1)} %copy.27), channel_id=1, replica_groups=mesh['row'=4,'col'=8] {'col'}, dimensions={0} | all-to-all | bytes 294912 | tf_op jit(solution)/shard_map/all_to_all | solution.py:77
  236.5 0.1 copy.30
  236.6 6.7 %all_gather.15 = bf16[144,2048]{1,0:T(8,128)(2,1)S(1)} all-gather(bf16[144,512]{1,0:T(8,128)(2,1)S(1)} %copy.30), channel_id=1, replica_groups=mesh['row'=4,'col'=8] {'row'}, dimensions={1}, use_global_device_ids=true | all-gather | bytes 737280 | tf_op jit(solution)/shard_map/all_gather | solution.py:79
  243.3 0.0 copy-start.6
  243.3 0.0 copy-start.7
  243.3 4.1 %fusion.3 = (f32[144]{0:T(256)S(1)}, f32[1076]{0:T(1024)S(1)}, f32[144,1076]{1,0:T(8,128)S(1)}) fusion(bf16[144,2048]{1,0:T(8,128)(2,1)S(1)} %all_gather.15, bf16[2048,1076]{0,1:T(8,128)(2,1)} %bitcast.36), kind=kOutput, calls=%fused_computation.9 | convolution fusion | flops 635269184 | bytes 5621776 | tf_op jit(solution)/shard_map/dot_general | solution.py:78
  247.3 16.7 %psum.29 = f32[1076]{0:T(1024)S(1)} all-reduce(f32[1076]{0:T(1024)S(1)} %get-tuple-element.5), channel_id=1, replica_groups=mesh['row'=4,'col'=8] {'col'}, use_global_device_ids=true, to_apply=%region_8.9 | all-reduce | flops 1076 | bytes 8608 | tf_op jit(solution)/shard_map/psum | solution.py:85
  264.0 5.7 %psum.28 = f32[144]{0:T(256)S(1)} all-reduce(f32[144]{0:T(256)S(1)} %get-tuple-element.4), channel_id=1, replica_groups=mesh['row'=4,'col'=8] {'row'}, use_global_device_ids=true, to_apply=%region_6.7 | all-reduce | flops 144 | bytes 1152 | tf_op jit(solution)/shard_map/psum | solution.py:84
  269.7 0.0 copy-done.6
  269.7 0.0 copy-done.7
  269.7 0.0 copy-start.4
  269.7 0.0 copy-start.5
  269.7 0.9 multiply_reduce_fusion
  270.7 44.0 %all-reduce = (f32[]{:T(128)}, f32[]{:T(128)}) all-reduce(f32[]{:T(128)} %multiply_reduce_fusion, f32[]{:T(128)} %get-tuple-element.9), channel_id=1, replica_groups=mesh['row'=4,'col'=8] {'row','col'}, use_global_device_ids=true, to_apply=%region_10.11 | all-reduce | flops 2 | bytes 16 | tf_op jit(solution)/shard_map/psum | solution.py:91
  315.4 1.0 fusion.4
  317.0 0.0 copy-done.4
  317.0 0.0 copy-done.5
  (7 shorter events, 0.1 us)
Async XLA Ops:
  7.2 93.2 %all-gather.3.cloned.1.call-start = ((), (), s32[]{:S(2)}) async-start(), calls=%async_computation.5 | async-start | bytes 5308416 | tf_op jit(solution)/shard_map/all_gather | solution.py:45
  22.2 124.2 %reduce-scatter.3.cloned.1.call-start = ((), (), s32[]{:S(2)}) async-start(), calls=%async_computation.6 | async-start | bytes 1474560 | tf_op jit(solution)/shard_map/reduce_scatter | solution.py:51
  114.6 3.9 %copy-start.2 = (f32[144,1076]{1,0:T(8,128)S(1)}, f32[144,1076]{1,0:T(8,128)}, u32[]{:S(2)}) copy-start(f32[144,1076]{1,0:T(8,128)} %param.11) | copy-start | bytes 1859332
  116.5 2.0 copy-start
  120.8 0.9 copy-start.3
  120.8 69.8 %all-gather.5.cloned.1.call-start = ((), (), s32[]{:S(2)}) async-start(), calls=%async_computation.7 | async-start | bytes 1327104 | tf_op jit(solution)/shard_map/all_gather | solution.py:66
  148.3 21.8 %all-to-all-start.1 = ((f32[144,8,64]{0,2,1:T(8,128)}), f32[144,8,64]{0,2,1:T(8,128)S(1)}, u32[]{:S(2)}, u32[]{:S(2)}) async-start(f32[144,8,64]{0,2,1:T(8,128)} %bitcast.1), calls=%async_computation.2 | async-start | bytes 1048576 | tf_op jit(solution)/shard_map/all_to_all | solution.py:52
  154.4 16.3 %copy-start.1 = (bf16[64,1152]{1,0:T(8,128)(2,1)S(1)}, bf16[64,1152]{1,0:T(8,128)(2,1)}, u32[]{:S(2)}) copy-start(bf16[64,1152]{1,0:T(8,128)(2,1)} %param.8) | copy-start | bytes 442372
  154.4 66.8 %reduce-scatter.5.cloned.1.call-start = ((), (), s32[]{:S(2)}) async-start(), calls=%async_computation.8 | async-start | bytes 1474560 | tf_op jit(solution)/shard_map/reduce_scatter | solution.py:73
  190.6 2.9 copy-start.8
  243.3 26.4 %copy-start.6 = (f32[1076]{0:T(1024)S(1)}, f32[1076]{0:T(1024)}, u32[]{:S(2)}) copy-start(f32[1076]{0:T(1024)} %param.13) | copy-start | bytes 12916
  243.3 26.4 %copy-start.7 = (f32[144]{0:T(256)S(1)}, f32[144]{0:T(256)}, u32[]{:S(2)}) copy-start(f32[144]{0:T(256)} %param.12) | copy-start | bytes 1732
  269.7 47.3 %copy-start.4 = (f32[1076]{0:T(1024)}, f32[1076]{0:T(1024)S(1)}, u32[]{:S(2)}) copy-start(f32[1076]{0:T(1024)S(1)} %multiply_add_fusion.1) | copy-start | bytes 12916
  269.7 47.3 %copy-start.5 = (f32[144]{0:T(256)}, f32[144]{0:T(256)S(1)}, u32[]{:S(2)}) copy-start(f32[144]{0:T(256)S(1)} %multiply_add_fusion.2) | copy-start | bytes 1732
Sparse Core Ops, SparseCore 0:
  22.3 78.0 all-gather.2
  120.9 25.4 reduce-scatter.2
  148.6 41.9 all-gather.4
  195.3 25.9 reduce-scatter.4
where the time goes:
time: 326 us; the launch traced here: 325 us
  waiting for transfers between devices  155 us (48%)
  blocking collectives  105 us (32%)
  local copies, waits for them, and re-layouts  24.9 us (8%)
  between operations  17.8 us (5%)
  matrix products  10.8 us (3%)
  starting transfers between devices  6.18 us (2%)
  other arithmetic  5.36 us (2%)
    all_gather x1, waiting for transfers between devices, per_device(): lax.all_gather(grouped, 'col', axis=1, tiled=True)  78.1 us
    psum x1, blocking collectives, per_device(): update_total = lax.psum(jnp.sum(raw_update * raw_update), ('row', 'col'))  44 us
    reduce_scatter x1, waiting for transfers between devices, per_device(): lax.psum_scatter(unit_part, 'row', scatter_dimension=0, tiled=True)  26.1 us
    reduce_scatter x1, waiting for transfers between devices, per_device(): lax.psum_scatter(partial_proj, 'row', scatter_dimension=1, tiled=True)  23.8 us
    psum x1, blocking collectives, per_device(): col_sum = lax.psum(jnp.sum(squared, axis=0), 'col')  16.7 us
    all_to_all x1, waiting for transfers between devices, per_device(): lax.all_to_all(summed, 'col', split_axis=1, concat_axis=0, tiled=True)  14.4 us
    all_to_all x1, blocking collectives, per_device(): lax.all_to_all(mixed_grad.T, 'col', split_axis=0, concat_axis=1, tiled=True)  12.6 us
    all_gather x1, waiting for transfers between devices, per_device(): piece = lax.all_gather(text_units, 'col', axis=0, tiled=True)  12.6 us
  transfers between devices with their start and end apart: 5, of which 5 were waited for; matrix products, arithmetic and copies ran while one was open for 1% of the time, Pallas kernels for 0%

commit v1 on v0

--- a/solution.py
+++ b/solution.py
@@ -82,7 +82,9 @@
     )
     squared = gradient * gradient + FLOOR_VALUE
     row_sum = lax.psum(jnp.sum(squared, axis=1), "row")
-    col_sum = lax.psum(jnp.sum(squared, axis=0), "col")
+    part = jnp.sum(squared, axis=0)
+    shards = lax.all_gather(part, "col")
+    col_sum = jnp.sum(shards, axis=0)
     new_row = DECAY_RATE * row_moment + (1.0 - DECAY_RATE) * row_sum / FF
     new_col = DECAY_RATE * col_moment + (1.0 - DECAY_RATE) * col_sum / D
     second = new_row[:, None] * new_col[None, :]

time: 326 us -> 343 us (1.052)
  starting transfers between devices: 6.18 us -> 12.2 us
  waiting for transfers between devices: 155 us -> 160 us
    unnamed x0 -> x1, blocking collectives: none -> 30.8 us
    psum x1 -> x0, blocking collectives: 16.7 us -> none  [per_device(): col_sum = lax.psum(jnp.sum(squared, axis=0), 'col')]
    all_to_all x1 -> x0, blocking collectives: 12.6 us -> none  [per_device(): lax.all_to_all(mixed_grad.T, 'col', split_axis=0, concat_axis=1, tiled=True)]
    all_to_all x0 -> x1, starting transfers between devices: none -> 6.02 us  [per_device(): lax.all_to_all(mixed_grad.T, 'col', split_axis=0, concat_axis=1, tiled=True)]
    all_to_all x0 -> x1, waiting for transfers between devices: none -> 5.53 us  [per_device(): lax.all_to_all(mixed_grad.T, 'col', split_axis=0, concat_axis=1, tiled=True)]
    unnamed x20 -> x25, local copies, waits for them, and re-layouts: 8.66 us -> 9.58 us
  transfers between devices with their start and end apart: 5 -> 6, of which waited for: 5 -> 6; matrix products, arithmetic and copies ran while one was open for 1% -> 1% of each run, Pallas kernels for 0% -> 0%
where the time goes in v1:
time: 343 us; the launch traced here: 342 us
  waiting for transfers between devices  160 us (47%)
  blocking collectives  108 us (31%)
  local copies, waits for them, and re-layouts  26.6 us (8%)
  between operations  18.4 us (5%)
  starting transfers between devices  12.2 us (4%)
  matrix products  10.8 us (3%)
  other arithmetic  5.38 us (2%)
    all_gather x1, waiting for transfers between devices, per_device(): lax.all_gather(grouped, 'col', axis=1, tiled=True)  78.1 us
    psum x1, blocking collectives, per_device(): update_total = lax.psum(jnp.sum(raw_update * raw_update), ('row', 'col'))  45.6 us
    unnamed x1, blocking collectives  30.8 us
    reduce_scatter x1, waiting for transfers between devices, per_device(): lax.psum_scatter(unit_part, 'row', scatter_dimension=0, tiled=True)  26.1 us
    reduce_scatter x1, waiting for transfers between devices, per_device(): lax.psum_scatter(partial_proj, 'row', scatter_dimension=1, tiled=True)  23.8 us
    all_to_all x1, waiting for transfers between devices, per_device(): lax.all_to_all(summed, 'col', split_axis=1, concat_axis=0, tiled=True)  14.4 us
    all_gather x1, waiting for transfers between devices, per_device(): piece = lax.all_gather(text_units, 'col', axis=0, tiled=True)  12.6 us
    all_to_all x1, blocking collectives, per_device(): lax.all_to_all(hidden, 'row', split_axis=1, concat_axis=0, tiled=True)  12.1 us
  transfers between devices with their start and end apart: 6, of which 6 were waited for; matrix products, arithmetic and copies ran while one was open for 1% of the time, Pallas kernels for 0%

profile of v1, /device:TPU:12, one launch (start us, length us, event | category | flops | bytes accessed | tf_op | source)
XLA Modules:
  0.0 341.8 jit_solution(15224812953323428541)
XLA Ops:
  7.2 0.0 all-gather.4.cloned.1.call-start
  7.2 1.5 all_to_all.40
  8.7 0.1 copy.29
  8.8 12.1 %all_to_all.54 = bf16[64,4,1076]{2,0,1:T(8,128)(2,1)S(1)} all-to-all(bf16[64,4,1076]{2,0,1:T(8,128)(2,1)S(1)} %copy.29), channel_id=1, replica_groups=mesh['row'=4,'col'=8] {'row'}, dimensions={1} | all-to-all | bytes 1101824 | tf_op jit(solution)/shard_map/all_to_all | solution.py:41
  20.9 1.3 copy.30
  22.1 0.0 all-gather.4.cloned.1.call-update
  22.2 0.0 reduce-scatter.3.cloned.1.call-start
  22.2 78.1 %all-gather.4.cloned.1.call-done = bf16[4,512,1076]{2,0,1:T(4,128)(2,1)} async-done(((bf16[4,64,1076]{2,0,1:T(4,128)(2,1)}), bf16[4,512,1076]{2,0,1:T(4,128)(2,1)}) %all-gather.4.cloned.1.call-update) | async-done | bytes 4407312 | tf_op jit(solution)/shard_map/all_gather | solution.py:45
  100.3 10.4 %copy.31 = bf16[4,512,1076]{1,0,2:T(4,128)(2,1)} copy(bf16[4,512,1076]{2,0,1:T(4,128)(2,1)} %all-gather.4.cloned.1.call-done) | data formatting | bytes 8814592 | tf_op jit(solution)/shard_map/all_gather | solution.py:45
  110.7 3.9 %pad = bf16[1080,4,512]{2,1,0:T(4,128)(2,1)S(1)} pad(bf16[1076,4,512]{2,1,0:T(4,128)(2,1)} %bitcast.39, bf16[]{:T(256)} %constant.85), padding=0_4x0_0x0_0 | pad | bytes 8830978
  114.6 0.0 copy-start.2
  114.6 1.9 copy.38
  116.5 0.0 copy-start
  116.5 2.0 copy-done
  118.5 0.0 copy-done.2
  118.5 2.2 fusion.6
  120.8 0.0 reduce-scatter.3.cloned.1.call-update
  120.8 0.0 all-gather.6.cloned.1.call-start
  120.9 0.8 copy-done.3
  121.7 0.1 fusion.8
  121.8 0.8 fusion.9
  122.6 0.0 all-gather.6.cloned.1.call-update
  122.6 23.8 %reduce-scatter.3.cloned.1.call-done = f32[144,512]{1,0:T(8,128)} async-done(((f32[144,2048]{1,0:T(8,128)}), f32[144,512]{1,0:T(8,128)}) %reduce-scatter.3.cloned.1.call-update) | async-done | bytes 294928 | tf_op jit(solution)/shard_map/reduce_scatter | solution.py:51
  146.4 2.0 copy.36
  148.3 6.1 %all-to-all-start.1 = ((f32[144,8,64]{0,2,1:T(8,128)}), f32[144,8,64]{0,2,1:T(8,128)S(1)}, u32[]{:S(2)}, u32[]{:S(2)}) async-start(f32[144,8,64]{0,2,1:T(8,128)} %bitcast.1), calls=%async_computation.2 | async-start | bytes 1048576 | tf_op jit(solution)/shard_map/all_to_all | solution.py:52
  154.4 0.0 reduce-scatter.5.cloned.1.call-start
  155.8 14.4 %all-to-all-done.1 = f32[144,8,64]{0,2,1:T(8,128)S(1)} async-done(((f32[144,8,64]{0,2,1:T(8,128)}), f32[144,8,64]{0,2,1:T(8,128)S(1)}, u32[]{:S(2)}, u32[]{:S(2)}) %all-to-all-start.1) | async-done | bytes 294944 | tf_op jit(solution)/shard_map/all_to_all | solution.py:52
  170.2 0.3 copy.33
  170.5 0.2 all_to_all.46
  170.7 0.0 copy-done.1
  170.7 0.1 multiply_reduce_fusion.2
  170.9 0.1 fusion.26
  171.0 7.1 %all_gather.19 = bf16[256,1152]{1,0:T(8,128)(2,1)S(1)} all-gather(bf16[64,1152]{1,0:T(8,128)(2,1)S(1)} %fusion.26), channel_id=1, replica_groups=mesh['row'=4,'col'=8] {'row'}, dimensions={0}, use_global_device_ids=true | all-gather | bytes 737280 | tf_op jit(solution)/shard_map/all_gather | solution.py:62
  178.1 12.6 %all-gather.6.cloned.1.call-done = bf16[512,1152]{1,0:T(8,128)(2,1)} async-done(((bf16[64,1152]{1,0:T(8,128)(2,1)}), bf16[512,1152]{1,0:T(8,128)(2,1)}) %all-gather.6.cloned.1.call-update) | async-done | bytes 1179664 | tf_op jit(solution)/shard_map/all_gather | solution.py:66
  190.6 2.9 fusion.5
  193.5 0.0 copy-done.8
  193.5 1.6 convolution_multiply_fusion
  195.1 0.0 reduce-scatter.5.cloned.1.call-update
  195.1 26.1 %reduce-scatter.5.cloned.1.call-done = f32[64,1152]{1,0:T(8,128)} async-done(((f32[256,1152]{1,0:T(8,128)}), f32[64,1152]{1,0:T(8,128)}) %reduce-scatter.5.cloned.1.call-update) | async-done | bytes 294928 | tf_op jit(solution)/shard_map/reduce_scatter | solution.py:73
  221.2 1.2 multiply_reduce_fusion.1
  222.4 0.0 copy-start.9
  222.4 1.1 fusion.16
  223.5 0.4 all_to_all.47
  223.9 0.8 copy.34
  224.6 6.0 %all-to-all-start.2 = ((bf16[8,144,64]{1,2,0:T(8,128)(2,1)}), bf16[8,144,64]{1,2,0:T(8,128)(2,1)S(1)}, u32[]{:S(2)}, u32[]{:S(2)}) async-start(bf16[8,144,64]{1,2,0:T(8,128)(2,1)} %copy.34), calls=%async_computation.4 | async-start | bytes 524288 | tf_op jit(solution)/shard_map/all_to_all | solution.py:77
  230.6 0.0 copy-done.9
  230.6 0.6 dynamic-slice
  231.9 5.5 %all-to-all-done.2 = bf16[8,144,64]{1,2,0:T(8,128)(2,1)S(1)} async-done(((bf16[8,144,64]{1,2,0:T(8,128)(2,1)}), bf16[8,144,64]{1,2,0:T(8,128)(2,1)S(1)}, u32[]{:S(2)}, u32[]{:S(2)}) %all-to-all-start.2) | async-done | bytes 147488 | tf_op jit(solution)/shard_map/all_to_all | solution.py:77
  237.4 0.1 copy.37
  237.5 6.7 %all_gather.21 = bf16[144,2048]{1,0:T(8,128)(2,1)S(1)} all-gather(bf16[144,512]{1,0:T(8,128)(2,1)S(1)} %copy.37), channel_id=1, replica_groups=mesh['row'=4,'col'=8] {'row'}, dimensions={1}, use_global_device_ids=true | all-gather | bytes 737280 | tf_op jit(solution)/shard_map/all_gather | solution.py:79
  244.2 4.1 %fusion.3 = (f32[144]{0:T(256)S(1)}, f32[1076]{0:T(1024)S(1)}, f32[144,1076]{1,0:T(8,128)S(1)}) fusion(bf16[144,2048]{1,0:T(8,128)(2,1)S(1)} %all_gather.21, bf16[2048,1076]{0,1:T(8,128)(2,1)} %bitcast.37), kind=kOutput, calls=%fused_computation.9 | convolution fusion | flops 635269184 | bytes 5621776 | tf_op jit(solution)/shard_map/dot_general | solution.py:78
  248.3 0.3 dynamic-update-slice
  248.6 30.8 %all-reduce = f32[8608]{0:T(1024)S(1)} all-reduce(f32[8608]{0:T(1024)S(1)} %dynamic-update-slice), channel_id=2, replica_groups=mesh['row'=4,'col'=8] {'col'}, use_global_device_ids=true, to_apply=%add | all-reduce | flops 8608 | bytes 68864
  279.4 0.1 reshape.66
  279.5 5.7 %psum.21 = f32[144]{0:T(256)S(1)} all-reduce(f32[144]{0:T(256)S(1)} %get-tuple-element.4), channel_id=1, replica_groups=mesh['row'=4,'col'=8] {'row'}, use_global_device_ids=true, to_apply=%region_6.7 | all-reduce | flops 144 | bytes 1152 | tf_op jit(solution)/shard_map/psum | solution.py:84
  285.2 0.0 copy-done.6
  285.2 0.0 copy-done.7
  285.2 0.0 copy-start.4
  285.2 0.0 copy-start.5
  285.2 0.9 multiply_reduce_fusion
  286.1 45.6 %all-reduce.1 = (f32[]{:T(128)}, f32[]{:T(128)}) all-reduce(f32[]{:T(128)} %multiply_reduce_fusion, f32[]{:T(128)} %get-tuple-element.9), channel_id=1, replica_groups=mesh['row'=4,'col'=8] {'row','col'}, use_global_device_ids=true, to_apply=%region_10.11 | all-reduce | flops 2 | bytes 16 | tf_op jit(solution)/shard_map/psum | solution.py:93
  332.5 1.0 fusion.4
  334.1 0.0 copy-done.4
  334.1 0.0 copy-done.5
  (13 shorter events, 0.1 us)
Async XLA Ops:
  7.2 93.2 %all-gather.4.cloned.1.call-start = ((), (), s32[]{:S(2)}) async-start(), calls=%async_computation.5 | async-start | bytes 5308416 | tf_op jit(solution)/shard_map/all_gather | solution.py:45
  22.2 124.2 %reduce-scatter.3.cloned.1.call-start = ((), (), s32[]{:S(2)}) async-start(), calls=%async_computation.6 | async-start | bytes 1474560 | tf_op jit(solution)/shard_map/reduce_scatter | solution.py:51
  114.6 3.9 %copy-start.2 = (f32[144,1076]{1,0:T(8,128)S(1)}, f32[144,1076]{1,0:T(8,128)}, u32[]{:S(2)}) copy-start(f32[144,1076]{1,0:T(8,128)} %param.11) | copy-start | bytes 1859332
  116.5 2.0 copy-start
  120.8 0.9 copy-start.3
  120.8 69.8 %all-gather.6.cloned.1.call-start = ((), (), s32[]{:S(2)}) async-start(), calls=%async_computation.7 | async-start | bytes 1327104 | tf_op jit(solution)/shard_map/all_gather | solution.py:66
  148.3 21.8 %all-to-all-start.1 = ((f32[144,8,64]{0,2,1:T(8,128)}), f32[144,8,64]{0,2,1:T(8,128)S(1)}, u32[]{:S(2)}, u32[]{:S(2)}) async-start(f32[144,8,64]{0,2,1:T(8,128)} %bitcast.1), calls=%async_computation.2 | async-start | bytes 1048576 | tf_op jit(solution)/shard_map/all_to_all | solution.py:52
  154.4 16.3 %copy-start.1 = (bf16[64,1152]{1,0:T(8,128)(2,1)S(1)}, bf16[64,1152]{1,0:T(8,128)(2,1)}, u32[]{:S(2)}) copy-start(bf16[64,1152]{1,0:T(8,128)(2,1)} %param.8) | copy-start | bytes 442372
  154.4 66.8 %reduce-scatter.5.cloned.1.call-start = ((), (), s32[]{:S(2)}) async-start(), calls=%async_computation.8 | async-start | bytes 1474560 | tf_op jit(solution)/shard_map/reduce_scatter | solution.py:73
  190.6 2.9 copy-start.8
  222.4 8.2 %copy-start.9 = (u32[32]{0:T(128)S(1)}, u32[32]{0:T(128)}, u32[]{:S(2)}) copy-start(u32[32]{0:T(128)} %constant.81) | copy-start | bytes 388
  224.6 12.8 %all-to-all-start.2 = ((bf16[8,144,64]{1,2,0:T(8,128)(2,1)}), bf16[8,144,64]{1,2,0:T(8,128)(2,1)S(1)}, u32[]{:S(2)}, u32[]{:S(2)}) async-start(bf16[8,144,64]{1,2,0:T(8,128)(2,1)} %copy.34), calls=%async_computation.4 | async-start | bytes 524288 | tf_op jit(solution)/shard_map/all_to_all | solution.py:77
  244.2 41.0 %copy-start.6 = (f32[1076]{0:T(1024)S(1)}, f32[1076]{0:T(1024)}, u32[]{:S(2)}) copy-start(f32[1076]{0:T(1024)} %param.13) | copy-start | bytes 12916
  244.2 41.0 %copy-start.7 = (f32[144]{0:T(256)S(1)}, f32[144]{0:T(256)}, u32[]{:S(2)}) copy-start(f32[144]{0:T(256)} %param.12) | copy-start | bytes 1732
  285.2 48.9 %copy-start.4 = (f32[1076]{0:T(1024)}, f32[1076]{0:T(1024)S(1)}, u32[]{:S(2)}) copy-start(f32[1076]{0:T(1024)S(1)} %multiply_add_fusion.1) | copy-start | bytes 12916
  285.2 48.9 %copy-start.5 = (f32[144]{0:T(256)}, f32[144]{0:T(256)S(1)}, u32[]{:S(2)}) copy-start(f32[144]{0:T(256)S(1)} %multiply_add_fusion.2) | copy-start | bytes 1732
Sparse Core Ops, SparseCore 0:
  22.3 78.0 all-gather.3
  120.9 25.4 reduce-scatter.2
  148.6 41.9 all-gather.5
  195.3 25.9 reduce-scatter.4
